TPU v7x, 32 devices: a whole 2x2x4 slice. The times are simulated.
32 devices in a mesh: row: 4 (over y, x), col: 8 (over z, core).
Axes of the slice: x: 2, y: 2, z: 4, core: 2. Of those that a mesh axis runs over, the one named last changes fastest.
Arguments:
- values: bfloat16 [4096, 4096], P('row', 'col'), may hold values from 0.0001296997 to 0.12988281
- tile_mask: int32 [32, 32], P('row', 'col'), may hold values 0 or 1
- keep_mask: int32 [32, 32], P('row', 'col'), may hold values 0 or 1
- thr_index: int32 [4096], P('col'), may hold values from 0 to 9
Outputs:
- expanded: bfloat16 [4096, 4096], P('row', 'col')
All inputs are finite; a program needn't handle non-finite values. No bound on the sum of `tile_mask` or of `keep_mask` on one device may be relied on, other than what follows from the above.
Results may differ from a plain program's by a relative error of at most 0.0004.
Values may be sent and summed in bfloat16 or wider, within the bound.
No kernel may reach another device: no remote copies, remote signals or barrier semaphores. Data moves between devices by JAX's collectives and lax.ppermute only.
A program may use at most 64 MiB of HBM per device.

v0:
```python
import functools

import jax
import jax.numpy as jnp
from jax import lax
from jax.experimental import pallas as pl
from jax.experimental.pallas import tpu as pltpu
from jax.sharding import PartitionSpec as P

TB = 128
PAD = 16
AXES = ("row", "col")
F32, BF16, I32 = jnp.float32, jnp.bfloat16, jnp.int32
VMEM = pl.BlockSpec(memory_space=pltpu.VMEM)
SMEM = pl.BlockSpec(memory_space=pltpu.SMEM)


def params(mib):
    return pltpu.CompilerParams(vmem_limit_bytes=mib * 1024 * 1024)


def cost(flops, moved):
    return pl.CostEstimate(flops=int(flops), bytes_accessed=int(moved), transcendentals=0)


def tiles_of(shape):
    return shape[0] // TB, shape[1] // TB


def place():
    col = lax.axis_index("col")
    return lax.axis_index("row"), col // 2, col % 2


def table_of(ref):
    end = ref.shape[0]
    return ref[end - PAD : end, :].astype(F32).astype(I32)[0:1, :]


def places(ref):
    return (ref.shape[0] - PAD) // TB


def pack_kernel(mask_in, block_in, head_ref, rest_ref, mask_ref, block_ref, mask_sem, sems):
    ti, tj = tiles_of(block_ref.shape)
    get_mask = pltpu.make_async_copy(mask_in, mask_ref, mask_sem)
    get_mask.start()
    chunk = block_ref.shape[0] // sems.shape[0]
    gets = []
    for k in range(sems.shape[0]):
        here = pl.ds(k * chunk, chunk)
        gets.append(pltpu.make_async_copy(block_in.at[here, :], block_ref.at[here, :], sems.at[k]))
        gets[-1].start()
    get_mask.wait()
    first, slots = places(head_ref), places(head_ref) + places(rest_ref)
    lane = lax.broadcasted_iota(I32, (PAD, TB), 1)
    table = jnp.full((PAD, TB), -1, I32)
    used = jnp.int32(0)
    for i in range(ti):
        if i * TB % chunk == 0:
            gets[i * TB // chunk].wait()
        for j in range(tj):
            stored = mask_ref[j, i]

            @pl.when(jnp.logical_and(stored > 0, used < first))
            def _(i=i, j=j, used=used):
                tile = block_ref[i * TB : (i + 1) * TB, j * TB : (j + 1) * TB]
                head_ref[pl.ds(pl.multiple_of(used * TB, TB), TB), :] = tile

            if i * tj + j >= first:

                @pl.when(jnp.logical_and(stored > 0, jnp.logical_and(used >= first, used < slots)))
                def _(i=i, j=j, used=used):
                    tile = block_ref[i * TB : (i + 1) * TB, j * TB : (j + 1) * TB]
                    rest_ref[pl.ds(pl.multiple_of((used - first) * TB, TB), TB), :] = tile

            table = jnp.where(lane == i * tj + j, jnp.where(stored > 0, used, -1), table)
            used = used + stored
    table = jnp.where(lane == ti * tj, used, table).astype(F32).astype(BF16)
    head_ref[first * TB :, :] = table
    rest_ref[(slots - first) * TB :, :] = table


def pack(block, mask_t, slots, first):
    return pl.pallas_call(
        pack_kernel,
        out_shape=tuple(jax.ShapeDtypeStruct((n * TB + PAD, TB), BF16) for n in (first, slots - first)),
        in_specs=[pl.BlockSpec(memory_space=pl.ANY)] * 2,
        out_specs=(VMEM, VMEM),
        scratch_shapes=[
            pltpu.SMEM(mask_t.shape, I32),
            pltpu.VMEM(block.shape, BF16),
            pltpu.SemaphoreType.DMA,
            pltpu.SemaphoreType.DMA((2,)),
        ],
        compiler_params=params(8),
        cost_estimate=cost(1e6, 2 * block.size * 2),
        name="pack",
    )(mask_t, block)


def load(ref, at, count):
    return ref[pl.ds(pl.multiple_of(jnp.clip(at, 0, count - 1) * TB, TB), TB), :]


def pool_kernel(first, mask_ref, block_ref, rest_ref, other_ref, out_ref, msg_ref):
    ti, tj = tiles_of(block_ref.shape)
    spare, n = places(rest_ref), out_ref.shape[0] // TB
    core = place()[2]
    count = jnp.int32(0)
    sums = [jnp.zeros((8, TB), F32) for _ in range(tj)]
    for i in range(ti):
        for j in range(tj):
            stored = mask_ref[j, i]
            count = count + stored
            tile = block_ref[i * TB : (i + 1) * TB, j * TB : (j + 1) * TB].astype(F32)
            sums[j] += jnp.sum(tile.reshape(TB // 8, 8, TB), axis=0) * stored.astype(F32)
    lane = lax.broadcasted_iota(I32, (1, TB), 1)
    theirs = jnp.max(jnp.where(lane == ti * tj, table_of(other_ref), 0))
    left = jnp.maximum(count - first, 0)
    left_other = jnp.maximum(theirs - first, 0)
    left_0 = jnp.where(core == 0, left, left_other)
    for i in range(n):
        p = core * n + i
        in_0 = p < left_0
        at = jnp.where(in_0, p, p - left_0)
        mine = jnp.where(in_0, 0, 1) == core
        tile = jnp.where(mine, load(rest_ref, at, spare), load(other_ref, at, spare))
        out_ref[i * TB : (i + 1) * TB, :] = tile
    over = jnp.logical_or(left > spare, left + left_other > 2 * n)
    msg_ref[...] = jnp.zeros_like(msg_ref)
    for j in range(tj):
        msg_ref[j : j + 1, :] = jnp.sum(sums[j], axis=0, keepdims=True)
    msg_ref[tj : tj + 1, :] = jnp.full((1, TB), 1.0, F32) * jnp.where(over, 1.0, 0.0)


def pool(block, mask_t, rest, other, first, n):
    s_rows = -(-(block.shape[1] // TB + 1) // 8) * 8
    return pl.pallas_call(
        functools.partial(pool_kernel, first),
        out_shape=(
            jax.ShapeDtypeStruct((n * TB, TB), BF16),
            jax.ShapeDtypeStruct((s_rows, TB), F32),
        ),
        in_specs=[SMEM] + [VMEM] * 3,
        out_specs=(VMEM, VMEM),
        compiler_params=params(8),
        cost_estimate=cost(1e6, 2 * block.size * 2),
        name="pool",
    )(mask_t, block, rest, other)


def start_tables(refs, itab, stab, sem):
    for q, ref in enumerate(refs):
        itab[q : q + 1, :] = table_of(ref)
    copy = pltpu.make_async_copy(itab, stab, sem)
    copy.start()
    return copy


def read_tables(refs, itab, stab, sem):
    start_tables(refs, itab, stab, sem).wait()


def zero_tile():
    return jnp.zeros((TB, TB), BF16)


def whole_tile(parts, at, low):
    first = places(parts[0])
    tile = load(parts[0], at, first)
    if not low:
        tile = jnp.where(at >= first, load(parts[1], at - first, places(parts[1])), tile)
    return jnp.where(at >= 0, tile, zero_tile())


def table_scratch(n):
    n8 = -(-n // 8) * 8
    return [pltpu.VMEM((n8, TB), I32), pltpu.SMEM((n8, TB), I32), pltpu.SemaphoreType.DMA]


def regroup(refs, sizes):
    out = []
    for s in sizes:
        out.append(refs[:s])
        refs = refs[s:]
    return out


def strip_rows(rows):
    return min(rows, 256)


def tile_getters(kind, refs, stab, at_table, tiles, core):
    first = places(refs[0])
    if kind == "whole":
        return [lambda at, low, b=b: whole_tile((refs[b], refs[2 + b]), at, low) for b in range(2)]

    def head(side, at):
        return jnp.where(
            jnp.logical_and(at >= 0, at < first), load(refs[side], at, first), zero_tile()
        )

    if kind == "heads":
        return [lambda at, low, b=b: head(b, at) for b in range(len(refs))]
    n = refs[2].shape[0] // TB
    left = [jnp.maximum(stab[at_table[b], tiles] - first, 0) for b in range(2)]
    left_0 = jnp.where(core == 0, left[0], left[1])

    def getter(side):
        base = jnp.where((core ^ side) == 1, left_0, 0) - first

        def get(at, low):
            if low:
                return head(side, at)
            p = at + base
            part = jnp.where(p >= n, 1, 0)
            local = p - part * n
            rest = jnp.where(part == core, load(refs[2], local, n), load(refs[3], local, n))
            if kind == "pools":
                return jnp.where(at >= first, rest, zero_tile())
            return jnp.where(at >= first, rest, head(side, at))

        return get

    return [getter(0), getter(1)]


def products(kind, refs, pair, panel_ref, stab, at_table, lhs, rows, use, sides=(0, 1), tables=None):
    cols = panel_ref.shape[1]
    step = strip_rows(rows)
    tj = cols // TB
    _, z, core = place()
    n = rows // step
    safe = places(refs[0]) // tj
    start = safe * TB // step if kind == "pools" else 0
    for m in range(start):
        use(m, None)
    if tables is not None:
        tables.wait()
    getters = tile_getters(kind, refs, stab, at_table, rows // TB * tj, core)

    def unpack(m):
        for b, get in enumerate(getters):
            for a in range(step // TB):
                i = m * (step // TB) + a
                tiles = [get(stab[at_table[b], i * tj + j], i < safe) for j in range(tj)]
                lhs[m % 2, a * TB : (a + 1) * TB, b * cols : (b + 1) * cols] = jnp.concatenate(tiles, axis=1)

    unpack(start)
    for m in range(start, n):
        if m + 1 < n:
            unpack(m + 1)
        total = None
        for b, side in enumerate(sides):
            at = pl.multiple_of((z ^ pair) * 2 * cols + (core ^ side) * cols, TB)
            got = jnp.dot(
                lhs[m % 2, :, b * cols : (b + 1) * cols],
                panel_ref[pl.ds(at, cols), :],
                preferred_element_type=F32,
            )
            total = got if total is None else total + got
        use(m, total)


def adder(acc_ref, prior_ref, rows):
    step = strip_rows(rows)

    def use(m, got):
        here = slice(m * step, (m + 1) * step)
        acc_ref[here, :] = got if prior_ref is None else prior_ref[here, :] + got

    return use


def dot_scratch(n, rows, cols):
    return table_scratch(n) + [pltpu.VMEM((2, strip_rows(rows), 2 * cols), BF16)]


def panel_kernel(n, rows, *refs):
    blocks, other = regroup(refs, [2] * n), refs[2 * n : 2 * n + 2]
    panel_ref, acc_ref, itab, stab, sem, lhs = refs[2 * n + 2 :]
    cols = panel_ref.shape[1]
    ti, tj = rows // TB, cols // TB
    me = place()[0]
    read_tables([b[1] for b in blocks] + [other[1]], itab, stab, sem)
    safe = places(blocks[0][0]) // tj
    for q in range(n):
        base = (me ^ q) * rows

        def strip(i, done, q=q, base=base, low=False):
            tiles = [whole_tile(blocks[q], stab[q, i * tj + j], low) for j in range(tj)]
            panel_ref[pl.ds(pl.multiple_of(base + i * TB, TB), TB), :] = jnp.concatenate(tiles, axis=1)
            return done

        lax.fori_loop(0, safe, functools.partial(strip, low=True), 0, unroll=2)
        lax.fori_loop(safe, ti, strip, 0, unroll=2)
    mine = blocks[0]
    heads_rests = (mine[0], other[0], mine[1], other[1])
    products("whole", heads_rests, 0, panel_ref, stab, (0, n), lhs, rows, adder(acc_ref, None, rows))


def panel(payloads, other, rows, cols):
    n = len(payloads)
    return pl.pallas_call(
        functools.partial(panel_kernel, n, rows),
        out_shape=(
            jax.ShapeDtypeStruct((n * rows, cols), BF16),
            jax.ShapeDtypeStruct((rows, cols), F32),
        ),
        in_specs=[VMEM] * (2 * n + 2),
        out_specs=(VMEM, VMEM),
        scratch_shapes=dot_scratch(n + 1, rows, cols),
        compiler_params=params(24),
        cost_estimate=cost(4 * rows * cols * cols, 2 * n * rows * cols * 2),
        name="panel",
    )(*[x for p in payloads for x in p], *other)


def dot_kernel(kind, pairs, rows, *refs):
    blocks = regroup(refs, [4] * len(pairs))
    panel_ref, prior_ref, acc_ref, itab, stab, sem, lhs = refs[4 * len(pairs) :]
    read_tables([r for b in blocks for r in b[:2]], itab, stab, sem)
    for k, (pair, b) in enumerate(zip(pairs, blocks)):
        use = adder(acc_ref, acc_ref if k else prior_ref, rows)
        products(kind, b, pair, panel_ref, stab, (2 * k, 2 * k + 1), lhs, rows, use)


def head_kernel(side, pair, rows, head_ref, panel_ref, prior_ref, acc_ref, itab, stab, sem, lhs):
    read_tables([head_ref], itab, stab, sem)
    use = adder(acc_ref, prior_ref, rows)
    products("heads", [head_ref], pair, panel_ref, stab, (0,), lhs, rows, use, sides=(side,))


def add_products(kernel, payloads, dense, prior, rows, n_tables):
    cols = dense.shape[1]
    return pl.pallas_call(
        kernel,
        out_shape=jax.ShapeDtypeStruct((rows, cols), F32),
        in_specs=[VMEM] * (len(payloads) + 2),
        out_specs=VMEM,
        scratch_shapes=dot_scratch(n_tables, rows, cols),
        input_output_aliases={len(payloads) + 1: 0},
        compiler_params=params(24),
        cost_estimate=cost(2 * rows * cols * cols * n_tables, 12 * rows * cols),
        name="dots",
    )(*payloads, dense, prior)


def dots(blocks, pairs, dense, prior, rows):
    kernel = functools.partial(dot_kernel, "all", pairs, rows)
    return add_products(kernel, [x for b in blocks for x in b], dense, prior, rows, 2 * len(pairs))


def head_dots(head, side, pair, dense, prior, rows):
    kernel = functools.partial(head_kernel, side, pair, rows)
    return add_products(kernel, [head], dense, prior, rows, 1)


def total_kernel(*refs):
    refs[-1][...] = functools.reduce(jnp.add, [r[...] for r in refs[:-1]])


def total_of(xs):
    return pl.pallas_call(
        total_kernel,
        out_shape=jax.ShapeDtypeStruct(xs[0].shape, F32),
        in_specs=[VMEM] * len(xs),
        out_specs=VMEM,
        compiler_params=params(4),
        cost_estimate=cost(1e5, 4 * xs[0].size * len(xs)),
        name="total",
    )(*xs)


def means_kernel(n_pairs, s_rows, order, *refs):
    msgs, (thr_ref, panel_ref, out_ref, flag_ref) = refs[:n_pairs], refs[n_pairs:]
    _, z, core = place()
    cols = panel_ref.shape[1]
    tj = cols // TB
    total = jnp.zeros((8, cols), F32)
    row = lax.broadcasted_iota(I32, (8, TB), 0)
    over = jnp.zeros((1, TB), F32)
    for q in range(n_pairs):
        for b in range(2):
            over = jnp.maximum(over, msgs[q][b * s_rows + tj : b * s_rows + tj + 1, :])
            for t in range(tj):
                s = jnp.broadcast_to(msgs[q][b * s_rows + t : b * s_rows + t + 1, :], (8, TB))
                high = s.astype(BF16).astype(F32)
                mid = (s - high).astype(BF16).astype(F32)
                low = s - high - mid
                lhs = jnp.where(row == 0, high, jnp.where(row == 1, mid, jnp.where(row == 2, low, 0.0)))
                at = (z ^ q) * 2 * cols + (core ^ b) * cols + t * TB
                total += jnp.dot(
                    lhs.astype(BF16),
                    panel_ref[pl.ds(pl.multiple_of(at, TB), TB), :],
                    preferred_element_type=F32,
                )
    mean = jnp.sum(total, axis=0, keepdims=True) / order
    out_ref[...] = jnp.broadcast_to(0.125 * thr_ref[...].astype(F32) * mean, out_ref.shape)
    flag_ref[0] = jnp.where(jnp.max(over) > 0.0, 1, 0).astype(I32)


def cuts_of(messages, thr, dense, s_rows, order):
    n = len(messages)
    cols = dense.shape[1]
    return pl.pallas_call(
        functools.partial(means_kernel, n, s_rows, order),
        out_shape=(jax.ShapeDtypeStruct((8, cols), F32), jax.ShapeDtypeStruct((1,), I32)),
        in_specs=[VMEM] * (n + 2),
        out_specs=(VMEM, SMEM),
        compiler_params=params(12),
        cost_estimate=cost(1e7, dense.size * 2),
        name="cuts",
    )(*messages, thr, dense)


def last_kernel(pair, rows, *refs):
    blocks, (panel_ref, prior_ref, cut_ref, keep_ref, acc_ref, tot_ref) = refs[:4], refs[4:10]
    itab, stab, sem, lhs = refs[10:]
    step = strip_rows(rows)
    cols = panel_ref.shape[1]
    per = step // TB
    totals = [jnp.zeros((8, cols), F32)]
    tables = start_tables(blocks[:2], itab, stab, sem)

    def use(m, got):
        prior = prior_ref[m * step : (m + 1) * step, :]
        got = jnp.maximum((prior if got is None else prior + got) - cut_ref[0:1, :], 0.0)
        for a in range(per):
            i = m * per + a
            cell = got[a * TB : (a + 1) * TB, :] * keep_ref[i : i + 1, :]
            acc_ref[i * TB : (i + 1) * TB, :] = cell
            totals[0] += jnp.sum(cell.reshape(TB // 8, 8, cols), axis=0)

    products("pools", blocks, pair, panel_ref, stab, (0, 1), lhs, rows, use, tables=tables)
    tot_ref[...] = jnp.sum(totals[0], axis=0, keepdims=True)


def finish(keep, blocks, pair, dense, prior, cut, rows):
    cols = dense.shape[1]
    return pl.pallas_call(
        functools.partial(last_kernel, pair, rows),
        out_shape=(jax.ShapeDtypeStruct((rows, cols), F32), jax.ShapeDtypeStruct((1, cols), F32)),
        in_specs=[VMEM] * 8,
        out_specs=(VMEM, VMEM),
        scratch_shapes=dot_scratch(2, rows, cols),
        compiler_params=params(20),
        cost_estimate=cost(4 * rows * cols * cols, 12 * rows * cols),
        name="finish",
    )(*blocks, dense, prior, cut, keep)


def scale_kernel(n, order, x_ref, *refs):
    tots, out_ref = refs[:n], refs[n]
    total = tots[0][...]
    for t in tots[1:]:
        total = total + t[...]
    total = total / order
    factor = 1.0 / jnp.maximum(total, 0.1)
    out_ref[...] = (x_ref[...] * factor).astype(BF16)


def scale(x, totals, order):
    n = len(totals)
    return pl.pallas_call(
        functools.partial(scale_kernel, n, order),
        out_shape=jax.ShapeDtypeStruct(x.shape, BF16),
        in_specs=[VMEM] * (n + 1),
        out_specs=VMEM,
        compiler_params=params(12),
        cost_estimate=cost(2 * x.size, 6 * x.size),
        name="scale",
    )(x, *totals)


def dense_path(values, tile_mask, keep_mask, thr_index, n_row, n_col):
    rows, cols = values.shape
    ti, tj = tiles_of(values.shape)
    matrix = (
        values.reshape(ti, TB, tj, TB) * tile_mask[:, None, :, None].astype(BF16)
    ).reshape(rows, cols)
    kept = jnp.broadcast_to(keep_mask[:, None, :, None].astype(F32), (ti, TB, tj, TB)).reshape(rows, cols)
    r, c = lax.axis_index("row"), lax.axis_index("col")
    order = rows * n_row

    def col_ring(i, carry):
        block, panel_ = carry
        panel_ = lax.dynamic_update_slice(panel_, block, (((r - i) % n_row) * rows, 0))
        return lax.ppermute(block, "row", [(k, (k + 1) % n_row) for k in range(n_row)]), panel_

    _, panel_ = lax.fori_loop(0, n_row, col_ring, (matrix, jnp.zeros((order, cols), BF16)))

    def row_ring(i, carry):
        block, acc = carry
        part = lax.dynamic_slice(panel_, (((c - i) % n_col) * cols, 0), (cols, cols))
        acc = acc + jnp.dot(block, part, preferred_element_type=F32)
        return lax.ppermute(block, "col", [(k, (k + 1) % n_col) for k in range(n_col)]), acc

    _, product = lax.fori_loop(0, n_col, row_ring, (matrix, jnp.zeros((rows, cols), F32)))
    means = lax.psum(jnp.sum(product, axis=0), "row") / order
    pruned = jnp.maximum(product - 0.125 * thr_index.astype(F32) * means, 0.0) * kept
    totals = lax.psum(jnp.sum(pruned, axis=0), "row") / order
    return (pruned / jnp.maximum(totals, 0.1)).astype(BF16)


def on_device(values, tile_mask, keep_mask, thr_index, n_row, n_col):
    return body(values, tile_mask, keep_mask, thr_index, n_row, n_col)


def body(values, tile_mask, keep_mask, thr_index, n_row, n_col):
    rows, cols = values.shape
    ti, tj = tiles_of(values.shape)
    first = ti * tj // 2
    extra = ti * tj * 3 // 16
    slots = ti * tj * 13 // 16
    n_z = n_col // 2
    last = n_z - 1
    order = rows * n_row

    def send(x, dr=0, dz=0, dc=0):
        pairs = [
            (r * n_col + z * 2 + c, (r ^ dr) * n_col + (z ^ dz) * 2 + (c ^ dc))
            for r in range(n_row)
            for z in range(n_z)
            for c in range(2)
        ]
        return lax.ppermute(x, AXES, pairs)

    own = pack(values, tile_mask.T, slots, first)
    own_swapped = [send(x, dc=1) for x in own]
    spare, sums = pool(values, tile_mask.T, own[1], own_swapped[1], first, extra)

    line = {0: [own[0], spare]}
    swapped = {}
    for j in range(1, n_z):
        low = j & -j
        line[j] = [send(x, dz=low) for x in line[j ^ low]]
        swapped[j] = [send(x, dc=1) for x in line[j]]

    column = {0: own}
    for q in range(1, n_row):
        low = q & -q
        rest = q ^ low
        if rest and rest & -rest == rest:
            column[q] = [send(column[low][0], dr=rest), send(column[rest][1], dr=low)]
        else:
            column[q] = [send(x, dr=q) for x in own]

    dense, acc = panel([column[q] for q in range(n_row)], own_swapped, rows, cols)

    sums = [sums] + [send(sums, dr=q) for q in range(1, n_row)]
    sums = total_of(sums)
    both = jnp.concatenate([sums, send(sums, dc=1)], axis=0)
    messages = [both] + [send(both, dz=j) for j in range(1, n_z)]
    cut, over = cuts_of(messages, thr_index.reshape(1, cols), dense, sums.shape[0], order)

    early = tuple(range(1, last))
    if early:
        blocks = [(line[j][0], swapped[j][0], line[j][1], swapped[j][1]) for j in early]
        acc = dots(blocks, early, dense, acc, rows)
    acc = head_dots(line[last][0], 0, last, dense, acc, rows)
    acc = head_dots(swapped[last][0], 1, last, dense, acc, rows)
    keep = jnp.repeat(keep_mask.astype(F32), TB, axis=1)

    def fast():
        blocks = (line[last][0], swapped[last][0], line[last][1], swapped[last][1])
        pruned, tot = finish(keep, blocks, last, dense, acc, cut, rows)
        totals = {0: tot}
        for q in range(1, n_row):
            low = q & -q
            totals[q] = send(totals[q ^ low], dr=low)
        totals = list(totals.values())
        return scale(pruned, totals, order)

    def full():
        return dense_path(values, tile_mask, keep_mask, thr_index, n_row, n_col)

    return lax.cond(over[0] > 0, full, fast)


def solution(mesh):
    n_row, n_col = mesh.shape["row"], mesh.shape["col"]
    return jax.shard_map(
        functools.partial(on_device, n_row=n_row, n_col=n_col),
        mesh=mesh,
        in_specs=(P("row", "col"), P("row", "col"), P("row", "col"), P("col")),
        out_specs=P("row", "col"),
        check_vma=False,
    )
```

profile of v0, /device:TPU:0, one launch (start us, length us, event | category | flops | bytes accessed | tf_op | source)
XLA Modules:
  0.0 98.8 jit_solution(13939661147184051913)
XLA Ops:
  0.0 1.5 %pack.1 = (bf16[2064,128]{1,0:T(8,128)(2,1)S(1)}, bf16[1296,128]{1,0:T(8,128)(2,1)S(1)}) custom-call(s32[4,8]{1,0:T(4,128)} %bitcast.29, bf16[1024,512]{1,0:T(8,128)(2,1)} %block_ref.1), custom_call_target="tpu_custom_call" | custom-call | flops 1000000 | bytes 2097152 | tf_op jit(solution)/shard_map/pack/pallas_call | solution.py:85
  2.1 2.6 %collective-permute-start.16 = (bf16[1296,128]{1,0:T(8,128)(2,1)S(1)}, bf16[1296,128]{1,0:T(8,128)(2,1)S(1)}, u32[]{:S(2)}, u32[]{:S(2)}) collective-permute-start(bf16[1296,128]{1,0:T(8,128)(2,1)S(1)} %get-tuple-element.300.rest_ref.refs_1_), channel_id=1, source_target_pairs={{0,16},{1,17},{2,18},{3,19},{4,20},{5,21},{6,22},{7,23},{8,24},{9,... | collective-permute-start | bytes 995336 | tf_op jit(solution)/shard_map/ppermute | solution.py:528
  6.7 2.6 %collective-permute-start.20 = (bf16[2064,128]{1,0:T(8,128)(2,1)S(1)}, bf16[2064,128]{1,0:T(8,128)(2,1)S(1)}, u32[]{:S(2)}, u32[]{:S(2)}) collective-permute-start(bf16[2064,128]{1,0:T(8,128)(2,1)S(1)} %get-tuple-element.302.refs_0_), channel_id=1, source_target_pairs={{0,4},{1,5},{2,6},{3,7},{4,0},{5,1},{6,2},{7,3},{8,12},{9,13},{10,... | collective-permute-start | bytes 1585160 | tf_op jit(solution)/shard_map/ppermute | solution.py:528
  9.3 1.5 %pool.1 = (bf16[768,128]{1,0:T(8,128)(2,1)S(1)}, f32[8,128]{1,0:T(8,128)S(1)}) custom-call(s32[4,8]{1,0:T(4,128)} %bitcast.30, bf16[1024,512]{1,0:T(8,128)(2,1)} %block_ref.1, bf16[1296,128]{1,0:T(8,128)(2,1)S(1)} %get-tuple-element.300.rest_ref.refs_1_, bf16[1296,128]{1,0:T(8,128)(2,1)S(1)} %collective-permute-done.5.other_ref.refs_9_), custom_call_target="tpu_custom_call" | custom-call | flops 1000000 | bytes 2097152 | tf_op jit(solution)/shard_map/pool/pallas_call | solution.py:139
  10.8 1.6 %collective-permute-start.6 = (f32[8,128]{1,0:T(8,128)S(1)}, f32[8,128]{1,0:T(8,128)S(1)}, u32[]{:S(2)}, u32[]{:S(2)}) collective-permute-start(f32[8,128]{1,0:T(8,128)S(1)} %get-tuple-element.301.refs_0_), channel_id=1, source_target_pairs={{0,8},{1,9},{2,10},{3,11},{4,12},{5,13},{6,14},{7,15},{8,0},{9,1},... | collective-permute-start | bytes 12296 | tf_op jit(solution)/shard_map/ppermute | solution.py:528
  13.1 1.7 %collective-permute-start.7 = (f32[8,128]{1,0:T(8,128)S(1)}, f32[8,128]{1,0:T(8,128)S(1)}, u32[]{:S(2)}, u32[]{:S(2)}) collective-permute-start(f32[8,128]{1,0:T(8,128)S(1)} %get-tuple-element.301.refs_0_), channel_id=1, source_target_pairs={{0,16},{1,17},{2,18},{3,19},{4,20},{5,21},{6,22},{7,23},{8,24},{9,... | collective-permute-start | bytes 12296 | tf_op jit(solution)/shard_map/ppermute | solution.py:528
  14.8 11.1 %collective-permute-done.6.refs_1_ = f32[8,128]{1,0:T(8,128)S(1)} collective-permute-done((f32[8,128]{1,0:T(8,128)S(1)}, f32[8,128]{1,0:T(8,128)S(1)}, u32[]{:S(2)}, u32[]{:S(2)}) %collective-permute-start.6) | collective-permute-done | bytes 4128 | tf_op jit(solution)/shard_map/ppermute | solution.py:528
  27.4 1.5 %collective-permute-start.15 = (bf16[2064,128]{1,0:T(8,128)(2,1)S(1)}, bf16[2064,128]{1,0:T(8,128)(2,1)S(1)}, u32[]{:S(2)}, u32[]{:S(2)}) collective-permute-start(bf16[2064,128]{1,0:T(8,128)(2,1)S(1)} %get-tuple-element.302.refs_0_), channel_id=1, source_target_pairs={{0,16},{1,17},{2,18},{3,19},{4,20},{5,21},{6,22},{7,23},{8,24},{9,... | collective-permute-start | bytes 1585160 | tf_op jit(solution)/shard_map/ppermute | solution.py:528
  28.9 1.7 %collective-permute-done.8.refs_3_ = f32[8,128]{1,0:T(8,128)S(1)} collective-permute-done((f32[8,128]{1,0:T(8,128)S(1)}, f32[8,128]{1,0:T(8,128)S(1)}, u32[]{:S(2)}, u32[]{:S(2)}) %collective-permute-start.8) | collective-permute-done | bytes 4128 | tf_op jit(solution)/shard_map/ppermute | solution.py:528
  32.5 1.6 %collective-permute-start.26 = (bf16[2064,128]{1,0:T(8,128)(2,1)S(1)}, bf16[2064,128]{1,0:T(8,128)(2,1)S(1)}, u32[]{:S(2)}, u32[]{:S(2)}) collective-permute-start(bf16[2064,128]{1,0:T(8,128)(2,1)S(1)} %get-tuple-element.302.refs_0_), channel_id=1, source_target_pairs={{0,2},{1,3},{2,0},{3,1},{4,6},{5,7},{6,4},{7,5},{8,10},{9,11},{10,... | collective-permute-start | bytes 1585160 | tf_op jit(solution)/shard_map/ppermute | solution.py:528
  34.0 2.6 %collective-permute-start.23 = (bf16[768,128]{1,0:T(8,128)(2,1)S(1)}, bf16[768,128]{1,0:T(8,128)(2,1)S(1)}, u32[]{:S(2)}, u32[]{:S(2)}) collective-permute-start(bf16[768,128]{1,0:T(8,128)(2,1)S(1)} %get-tuple-element.305), channel_id=1, source_target_pairs={{0,4},{1,5},{2,6},{3,7},{4,0},{5,1},{6,2},{7,3},{8,12},{9,13},{10,... | collective-permute-start | bytes 589832 | tf_op jit(solution)/shard_map/ppermute | solution.py:528
  37.1 3.3 %collective-permute-done.15.refs_4_ = bf16[2064,128]{1,0:T(8,128)(2,1)S(1)} collective-permute-done((bf16[2064,128]{1,0:T(8,128)(2,1)S(1)}, bf16[2064,128]{1,0:T(8,128)(2,1)S(1)}, u32[]{:S(2)}, u32[]{:S(2)}) %collective-permute-start.15) | collective-permute-done | bytes 528416 | tf_op jit(solution)/shard_map/ppermute | solution.py:528
  42.4 8.2 %collective-permute-done.23.refs_6_ = bf16[768,128]{1,0:T(8,128)(2,1)S(1)} collective-permute-done((bf16[768,128]{1,0:T(8,128)(2,1)S(1)}, bf16[768,128]{1,0:T(8,128)(2,1)S(1)}, u32[]{:S(2)}, u32[]{:S(2)}) %collective-permute-start.23) | collective-permute-done | bytes 196640 | tf_op jit(solution)/shard_map/ppermute | solution.py:528
  50.7 3.5 %collective-permute-start.28 = (bf16[768,128]{1,0:T(8,128)(2,1)S(1)}, bf16[768,128]{1,0:T(8,128)(2,1)S(1)}, u32[]{:S(2)}, u32[]{:S(2)}) collective-permute-start(bf16[768,128]{1,0:T(8,128)(2,1)S(1)} %get-tuple-element.305), channel_id=1, source_target_pairs={{0,2},{1,3},{2,0},{3,1},{4,6},{5,7},{6,4},{7,5},{8,10},{9,11},{10,... | collective-permute-start | bytes 589832 | tf_op jit(solution)/shard_map/ppermute | solution.py:528
  54.1 12.1 %collective-permute-done.28.refs_2_ = bf16[768,128]{1,0:T(8,128)(2,1)S(1)} collective-permute-done((bf16[768,128]{1,0:T(8,128)(2,1)S(1)}, bf16[768,128]{1,0:T(8,128)(2,1)S(1)}, u32[]{:S(2)}, u32[]{:S(2)}) %collective-permute-start.28) | collective-permute-done | bytes 196640 | tf_op jit(solution)/shard_map/ppermute | solution.py:528
  67.3 1.9 %collective-permute-done.31.refs_7_ = bf16[768,128]{1,0:T(8,128)(2,1)S(1)} collective-permute-done((bf16[768,128]{1,0:T(8,128)(2,1)S(1)}, bf16[768,128]{1,0:T(8,128)(2,1)S(1)}, u32[]{:S(2)}, u32[]{:S(2)}) %collective-permute-start.31) | collective-permute-done | bytes 196640 | tf_op jit(solution)/shard_map/ppermute | solution.py:528
  69.2 1.6 %collective-permute-start.24 = (bf16[768,128]{1,0:T(8,128)(2,1)S(1)}, bf16[768,128]{1,0:T(8,128)(2,1)S(1)}, u32[]{:S(2)}, u32[]{:S(2)}) collective-permute-start(bf16[768,128]{1,0:T(8,128)(2,1)S(1)} %collective-permute-done.23.refs_6_), channel_id=1, source_target_pairs={{0,2},{1,3},{2,0},{3,1},{4,6},{5,7},{6,4},{7,5},{8,10},{9,11},{10,... | collective-permute-start | bytes 589832 | tf_op jit(solution)/shard_map/ppermute | solution.py:528
  70.8 3.4 %panel.1 = (bf16[4096,512]{1,0:T(8,128)(2,1)S(1)}, f32[1024,512]{1,0:T(8,128)S(1)}) custom-call(bf16[2064,128]{1,0:T(8,128)(2,1)S(1)} %get-tuple-element.302.refs_0_, bf16[1296,128]{1,0:T(8,128)(2,1)S(1)} %get-tuple-element.300.rest_ref.refs_1_, bf16[2064,128]{1,0:T(8,128)(2,1)S(1)} %collective-permute-done.13.refs_2_, ...), custom_call_target="tpu_custom_call" | custom-call | flops 1073741824 | bytes 8388608 | tf_op jit(solution)/shard_map/panel/pallas_call | solution.py:305
  76.2 2.6 %collective-permute-start.11 = (f32[16,128]{1,0:T(8,128)S(1)}, f32[16,128]{1,0:T(8,128)S(1)}, u32[]{:S(2)}, u32[]{:S(2)}) collective-permute-start(f32[16,128]{1,0:T(8,128)S(1)} %pad_maximum_fusion.refs_0_), channel_id=1, source_target_pairs={{0,4},{1,5},{2,6},{3,7},{4,0},{5,1},{6,2},{7,3},{8,12},{9,13},{10,... | collective-permute-start | bytes 24584 | tf_op jit(solution)/shard_map/ppermute | solution.py:528
  80.1 3.3 %dots.3.prior_ref = f32[1024,512]{1,0:T(8,128)S(1)} custom-call(bf16[2064,128]{1,0:T(8,128)(2,1)S(1)} %collective-permute-done.26.refs_0_, bf16[2064,128]{1,0:T(8,128)(2,1)S(1)} %collective-permute-done.27.refs_1_, bf16[768,128]{1,0:T(8,128)(2,1)S(1)} %collective-permute-done.28.refs_2_, ...), custom_call_target="tpu_custom_call", output_to_operand_aliasing={{}: (9, {})} | custom-call | flops 2147483648 | bytes 6291456 | tf_op jit(solution)/shard_map/dots/pallas_call | solution.py:337
  88.9 9.8 %conditional.1 = (bf16[1024,512]{1,0:T(8,128)(2,1)}) conditional(s32[]{:T(128)} %bitcast.3, (f32[8,4]{0,1:T(4,128)S(1)}, bf16[2064,128]{1,0:T(8,128)(2,1)S(1)}, bf16[2064,128]{1,0:T(8,128)(2,1)S(1)}, bf16[768,128]{1,0:T(8,128)(2,1)S(1)}, bf16[768,128]{1,0:T(8,128)(2,1)S(1)}, /*index=5*/bf16[4096,512]{1,0:T(8,128)(2,1)S(1)}, ...), branch_computations={%region_0.0_spmd, %region_1.10_spmd} | conditional | flops 1074790400 | bytes 55080728 | solution.py:579
  92.5 1.6 %collective-permute-done.1.refs_2_ = f32[1,512]{1,0:T(1,128)S(1)} collective-permute-done((f32[1,512]{1,0:T(1,128)S(1)}, f32[1,512]{1,0:T(1,128)S(1)}, u32[]{:S(2)}, u32[]{:S(2)}) %collective-permute-start.1) | collective-permute-done | bytes 2080 | tf_op jit(solution)/shard_map/cond/branch_0_fun/ppermute | solution.py:528
  94.1 1.5 %collective-permute-start.2 = (f32[1,512]{1,0:T(1,128)S(1)}, f32[1,512]{1,0:T(1,128)S(1)}, u32[]{:S(2)}, u32[]{:S(2)}) collective-permute-start(f32[1,512]{1,0:T(1,128)S(1)} %collective-permute-done.1.refs_2_), channel_id=1, source_target_pairs={{0,8},{1,9},{2,10},{3,11},{4,12},{5,13},{6,14},{7,15},{8,0},{9,1},... | collective-permute-start | bytes 6152 | tf_op jit(solution)/shard_map/cond/branch_0_fun/ppermute | solution.py:528
  95.6 2.1 %collective-permute-done.2.refs_3_ = f32[1,512]{1,0:T(1,128)S(1)} collective-permute-done((f32[1,512]{1,0:T(1,128)S(1)}, f32[1,512]{1,0:T(1,128)S(1)}, u32[]{:S(2)}, u32[]{:S(2)}) %collective-permute-start.2) | collective-permute-done | bytes 2080 | tf_op jit(solution)/shard_map/cond/branch_0_fun/ppermute | solution.py:528
  (58 shorter events, 22.9 us)
Async XLA Ops:
  1.5 7.7 %collective-permute-start.5 = (bf16[1296,128]{1,0:T(8,128)(2,1)S(1)}, bf16[1296,128]{1,0:T(8,128)(2,1)S(1)}, u32[]{:S(2)}, u32[]{:S(2)}) collective-permute-start(bf16[1296,128]{1,0:T(8,128)(2,1)S(1)} %get-tuple-element.300.rest_ref.refs_1_), channel_id=1, source_target_pairs={{0,1},{1,0},{2,3},{3,2},{4,5},{5,4},{6,7},{7,6},{8,9},{9,8},{10,11... | collective-permute-start | bytes 995336 | tf_op jit(solution)/shard_map/ppermute | solution.py:528
  2.1 11.0 %collective-permute-start.16 = (bf16[1296,128]{1,0:T(8,128)(2,1)S(1)}, bf16[1296,128]{1,0:T(8,128)(2,1)S(1)}, u32[]{:S(2)}, u32[]{:S(2)}) collective-permute-start(bf16[1296,128]{1,0:T(8,128)(2,1)S(1)} %get-tuple-element.300.rest_ref.refs_1_), channel_id=1, source_target_pairs={{0,16},{1,17},{2,18},{3,19},{4,20},{5,21},{6,22},{7,23},{8,24},{9,... | collective-permute-start | bytes 995336 | tf_op jit(solution)/shard_map/ppermute | solution.py:528
  4.7 29.4 %collective-permute-start.13 = (bf16[2064,128]{1,0:T(8,128)(2,1)S(1)}, bf16[2064,128]{1,0:T(8,128)(2,1)S(1)}, u32[]{:S(2)}, u32[]{:S(2)}) collective-permute-start(bf16[2064,128]{1,0:T(8,128)(2,1)S(1)} %get-tuple-element.302.refs_0_), channel_id=1, source_target_pairs={{0,8},{1,9},{2,10},{3,11},{4,12},{5,13},{6,14},{7,15},{8,0},{9,1},... | collective-permute-start | bytes 1585160 | tf_op jit(solution)/shard_map/ppermute | solution.py:528
  6.2 24.4 %collective-permute-start.14 = (bf16[1296,128]{1,0:T(8,128)(2,1)S(1)}, bf16[1296,128]{1,0:T(8,128)(2,1)S(1)}, u32[]{:S(2)}, u32[]{:S(2)}) collective-permute-start(bf16[1296,128]{1,0:T(8,128)(2,1)S(1)} %get-tuple-element.300.rest_ref.refs_1_), channel_id=1, source_target_pairs={{0,8},{1,9},{2,10},{3,11},{4,12},{5,13},{6,14},{7,15},{8,0},{9,1},... | collective-permute-start | bytes 995336 | tf_op jit(solution)/shard_map/ppermute | solution.py:528
  6.7 29.9 %collective-permute-start.20 = (bf16[2064,128]{1,0:T(8,128)(2,1)S(1)}, bf16[2064,128]{1,0:T(8,128)(2,1)S(1)}, u32[]{:S(2)}, u32[]{:S(2)}) collective-permute-start(bf16[2064,128]{1,0:T(8,128)(2,1)S(1)} %get-tuple-element.302.refs_0_), channel_id=1, source_target_pairs={{0,4},{1,5},{2,6},{3,7},{4,0},{5,1},{6,2},{7,3},{8,12},{9,13},{10,... | collective-permute-start | bytes 1585160 | tf_op jit(solution)/shard_map/ppermute | solution.py:528
  10.8 15.1 %collective-permute-start.6 = (f32[8,128]{1,0:T(8,128)S(1)}, f32[8,128]{1,0:T(8,128)S(1)}, u32[]{:S(2)}, u32[]{:S(2)}) collective-permute-start(f32[8,128]{1,0:T(8,128)S(1)} %get-tuple-element.301.refs_0_), channel_id=1, source_target_pairs={{0,8},{1,9},{2,10},{3,11},{4,12},{5,13},{6,14},{7,15},{8,0},{9,1},... | collective-permute-start | bytes 12296 | tf_op jit(solution)/shard_map/ppermute | solution.py:528
  13.1 14.3 %collective-permute-start.7 = (f32[8,128]{1,0:T(8,128)S(1)}, f32[8,128]{1,0:T(8,128)S(1)}, u32[]{:S(2)}, u32[]{:S(2)}) collective-permute-start(f32[8,128]{1,0:T(8,128)S(1)} %get-tuple-element.301.refs_0_), channel_id=1, source_target_pairs={{0,16},{1,17},{2,18},{3,19},{4,20},{5,21},{6,22},{7,23},{8,24},{9,... | collective-permute-start | bytes 12296 | tf_op jit(solution)/shard_map/ppermute | solution.py:528
  26.0 4.6 %collective-permute-start.8 = (f32[8,128]{1,0:T(8,128)S(1)}, f32[8,128]{1,0:T(8,128)S(1)}, u32[]{:S(2)}, u32[]{:S(2)}) collective-permute-start(f32[8,128]{1,0:T(8,128)S(1)} %get-tuple-element.301.refs_0_), channel_id=1, source_target_pairs={{0,24},{1,25},{2,26},{3,27},{4,28},{5,29},{6,30},{7,31},{8,16},{9,... | collective-permute-start | bytes 12296 | tf_op jit(solution)/shard_map/ppermute | solution.py:528
  27.4 13.0 %collective-permute-start.15 = (bf16[2064,128]{1,0:T(8,128)(2,1)S(1)}, bf16[2064,128]{1,0:T(8,128)(2,1)S(1)}, u32[]{:S(2)}, u32[]{:S(2)}) collective-permute-start(bf16[2064,128]{1,0:T(8,128)(2,1)S(1)} %get-tuple-element.302.refs_0_), channel_id=1, source_target_pairs={{0,16},{1,17},{2,18},{3,19},{4,20},{5,21},{6,22},{7,23},{8,24},{9,... | collective-permute-start | bytes 1585160 | tf_op jit(solution)/shard_map/ppermute | solution.py:528
  30.6 10.4 %collective-permute-start.19 = (bf16[2064,128]{1,0:T(8,128)(2,1)S(1)}, bf16[2064,128]{1,0:T(8,128)(2,1)S(1)}, u32[]{:S(2)}, u32[]{:S(2)}) collective-permute-start(bf16[2064,128]{1,0:T(8,128)(2,1)S(1)} %get-tuple-element.302.refs_0_), channel_id=1, source_target_pairs={{0,1},{1,0},{2,3},{3,2},{4,5},{5,4},{6,7},{7,6},{8,9},{9,8},{10,11... | collective-permute-start | bytes 1585160 | tf_op jit(solution)/shard_map/ppermute | solution.py:528
  32.5 33.8 %collective-permute-start.26 = (bf16[2064,128]{1,0:T(8,128)(2,1)S(1)}, bf16[2064,128]{1,0:T(8,128)(2,1)S(1)}, u32[]{:S(2)}, u32[]{:S(2)}) collective-permute-start(bf16[2064,128]{1,0:T(8,128)(2,1)S(1)} %get-tuple-element.302.refs_0_), channel_id=1, source_target_pairs={{0,2},{1,3},{2,0},{3,1},{4,6},{5,7},{6,4},{7,5},{8,10},{9,11},{10,... | collective-permute-start | bytes 1585160 | tf_op jit(solution)/shard_map/ppermute | solution.py:528
  34.0 16.6 %collective-permute-start.23 = (bf16[768,128]{1,0:T(8,128)(2,1)S(1)}, bf16[768,128]{1,0:T(8,128)(2,1)S(1)}, u32[]{:S(2)}, u32[]{:S(2)}) collective-permute-start(bf16[768,128]{1,0:T(8,128)(2,1)S(1)} %get-tuple-element.305), channel_id=1, source_target_pairs={{0,4},{1,5},{2,6},{3,7},{4,0},{5,1},{6,2},{7,3},{8,12},{9,13},{10,... | collective-permute-start | bytes 589832 | tf_op jit(solution)/shard_map/ppermute | solution.py:528
  36.6 30.3 %collective-permute-start.21 = (bf16[2064,128]{1,0:T(8,128)(2,1)S(1)}, bf16[2064,128]{1,0:T(8,128)(2,1)S(1)}, u32[]{:S(2)}, u32[]{:S(2)}) collective-permute-start(bf16[2064,128]{1,0:T(8,128)(2,1)S(1)} %collective-permute-done.20.refs_4_), channel_id=1, source_target_pairs={{0,2},{1,3},{2,0},{3,1},{4,6},{5,7},{6,4},{7,5},{8,10},{9,11},{10,... | collective-permute-start | bytes 1585160 | tf_op jit(solution)/shard_map/ppermute | solution.py:528
  40.4 26.4 %collective-permute-start.18 = (bf16[1296,128]{1,0:T(8,128)(2,1)S(1)}, bf16[1296,128]{1,0:T(8,128)(2,1)S(1)}, u32[]{:S(2)}, u32[]{:S(2)}) collective-permute-start(bf16[1296,128]{1,0:T(8,128)(2,1)S(1)} %collective-permute-done.16.refs_5_), channel_id=1, source_target_pairs={{0,8},{1,9},{2,10},{3,11},{4,12},{5,13},{6,14},{7,15},{8,0},{9,1},... | collective-permute-start | bytes 995336 | tf_op jit(solution)/shard_map/ppermute | solution.py:528
  40.9 29.9 %collective-permute-start.17 = (bf16[2064,128]{1,0:T(8,128)(2,1)S(1)}, bf16[2064,128]{1,0:T(8,128)(2,1)S(1)}, u32[]{:S(2)}, u32[]{:S(2)}) collective-permute-start(bf16[2064,128]{1,0:T(8,128)(2,1)S(1)} %collective-permute-done.13.refs_2_), channel_id=1, source_target_pairs={{0,16},{1,17},{2,18},{3,19},{4,20},{5,21},{6,22},{7,23},{8,24},{9,... | collective-permute-start | bytes 1585160 | tf_op jit(solution)/shard_map/ppermute | solution.py:528
  50.7 15.6 %collective-permute-start.28 = (bf16[768,128]{1,0:T(8,128)(2,1)S(1)}, bf16[768,128]{1,0:T(8,128)(2,1)S(1)}, u32[]{:S(2)}, u32[]{:S(2)}) collective-permute-start(bf16[768,128]{1,0:T(8,128)(2,1)S(1)} %get-tuple-element.305), channel_id=1, source_target_pairs={{0,2},{1,3},{2,0},{3,1},{4,6},{5,7},{6,4},{7,5},{8,10},{9,11},{10,... | collective-permute-start | bytes 589832 | tf_op jit(solution)/shard_map/ppermute | solution.py:528
  66.3 12.5 %collective-permute-start.30 = (bf16[2064,128]{1,0:T(8,128)(2,1)S(1)}, bf16[2064,128]{1,0:T(8,128)(2,1)S(1)}, u32[]{:S(2)}, u32[]{:S(2)}) collective-permute-start(bf16[2064,128]{1,0:T(8,128)(2,1)S(1)} %collective-permute-done.20.refs_4_), channel_id=1, source_target_pairs={{0,1},{1,0},{2,3},{3,2},{4,5},{5,4},{6,7},{7,6},{8,9},{9,8},{10,11... | collective-permute-start | bytes 1585160 | tf_op jit(solution)/shard_map/ppermute | solution.py:528
  66.3 13.8 %collective-permute-start.27 = (bf16[2064,128]{1,0:T(8,128)(2,1)S(1)}, bf16[2064,128]{1,0:T(8,128)(2,1)S(1)}, u32[]{:S(2)}, u32[]{:S(2)}) collective-permute-start(bf16[2064,128]{1,0:T(8,128)(2,1)S(1)} %collective-permute-done.26.refs_0_), channel_id=1, source_target_pairs={{0,1},{1,0},{2,3},{3,2},{4,5},{5,4},{6,7},{7,6},{8,9},{9,8},{10,11... | collective-permute-start | bytes 1585160 | tf_op jit(solution)/shard_map/ppermute | solution.py:528
  66.9 20.6 %collective-permute-start.22 = (bf16[2064,128]{1,0:T(8,128)(2,1)S(1)}, bf16[2064,128]{1,0:T(8,128)(2,1)S(1)}, u32[]{:S(2)}, u32[]{:S(2)}) collective-permute-start(bf16[2064,128]{1,0:T(8,128)(2,1)S(1)} %collective-permute-done.21.head_ref), channel_id=1, source_target_pairs={{0,1},{1,0},{2,3},{3,2},{4,5},{5,4},{6,7},{7,6},{8,9},{9,8},{10,11... | collective-permute-start | bytes 1585160 | tf_op jit(solution)/shard_map/ppermute | solution.py:528
  69.2 6.9 %collective-permute-start.24 = (bf16[768,128]{1,0:T(8,128)(2,1)S(1)}, bf16[768,128]{1,0:T(8,128)(2,1)S(1)}, u32[]{:S(2)}, u32[]{:S(2)}) collective-permute-start(bf16[768,128]{1,0:T(8,128)(2,1)S(1)} %collective-permute-done.23.refs_6_), channel_id=1, source_target_pairs={{0,2},{1,3},{2,0},{3,1},{4,6},{5,7},{6,4},{7,5},{8,10},{9,11},{10,... | collective-permute-start | bytes 589832 | tf_op jit(solution)/shard_map/ppermute | solution.py:528
  74.2 9.2 %collective-permute-start.10 = (f32[16,128]{1,0:T(8,128)S(1)}, f32[16,128]{1,0:T(8,128)S(1)}, u32[]{:S(2)}, u32[]{:S(2)}) collective-permute-start(f32[16,128]{1,0:T(8,128)S(1)} %pad_maximum_fusion.refs_0_), channel_id=1, source_target_pairs={{0,2},{1,3},{2,0},{3,1},{4,6},{5,7},{6,4},{7,5},{8,10},{9,11},{10,... | collective-permute-start | bytes 24584 | tf_op jit(solution)/shard_map/ppermute | solution.py:528
  76.2 7.3 %collective-permute-start.11 = (f32[16,128]{1,0:T(8,128)S(1)}, f32[16,128]{1,0:T(8,128)S(1)}, u32[]{:S(2)}, u32[]{:S(2)}) collective-permute-start(f32[16,128]{1,0:T(8,128)S(1)} %pad_maximum_fusion.refs_0_), channel_id=1, source_target_pairs={{0,4},{1,5},{2,6},{3,7},{4,0},{5,1},{6,2},{7,3},{8,12},{9,13},{10,... | collective-permute-start | bytes 24584 | tf_op jit(solution)/shard_map/ppermute | solution.py:528
  78.7 5.4 %collective-permute-start.12 = (f32[16,128]{1,0:T(8,128)S(1)}, f32[16,128]{1,0:T(8,128)S(1)}, u32[]{:S(2)}, u32[]{:S(2)}) collective-permute-start(f32[16,128]{1,0:T(8,128)S(1)} %pad_maximum_fusion.refs_0_), channel_id=1, source_target_pairs={{0,6},{1,7},{2,4},{3,5},{4,2},{5,3},{6,0},{7,1},{8,14},{9,15},{10,... | collective-permute-start | bytes 24584 | tf_op jit(solution)/shard_map/ppermute | solution.py:528
  80.1 8.8 %collective-permute-start.25 = (bf16[768,128]{1,0:T(8,128)(2,1)S(1)}, bf16[768,128]{1,0:T(8,128)(2,1)S(1)}, u32[]{:S(2)}, u32[]{:S(2)}) collective-permute-start(bf16[768,128]{1,0:T(8,128)(2,1)S(1)} %collective-permute-done.24), channel_id=1, source_target_pairs={{0,1},{1,0},{2,3},{3,2},{4,5},{5,4},{6,7},{7,6},{8,9},{9,8},{10,11... | collective-permute-start | bytes 589832 | tf_op jit(solution)/shard_map/ppermute | solution.py:528
  (10 other events, 93.9 us)
where the time goes:
time: 98.9 us; the launch traced here: 98.8 us
  waiting for transfers between devices  46.3 us (47%)
  starting transfers between devices  35.3 us (36%)
  Pallas kernels  16.3 us (16%)
    ppermute x30, waiting for transfers between devices, send(): return lax.ppermute(x, AXES, pairs)  46.3 us
    ppermute x30, starting transfers between devices, send(): return lax.ppermute(x, AXES, pairs)  35.3 us
    pallas_call x3, Pallas kernels, add_products(): pl.pallas_call(kernel, out_shape=jax.ShapeDtypeStruct((rows, cols), F32),...  6.2 us
    pallas_call x1, Pallas kernels, panel(): pl.pallas_call(functools.partial(panel_kernel, n, rows), out_shape=(jax.S...  3.38 us
  transfers between devices with their start and end apart: 30, of which 12 were waited for; matrix products, arithmetic and copies ran while one was open for 0% of the time, Pallas kernels for 12%

commit v1 on v0

--- a/solution.py
+++ b/solution.py
@@ -566,12 +566,11 @@
     def fast():
         blocks = (line[last][0], swapped[last][0], line[last][1], swapped[last][1])
         pruned, tot = finish(keep, blocks, last, dense, acc, cut, rows)
-        totals = {0: tot}
-        for q in range(1, n_row):
-            low = q & -q
-            totals[q] = send(totals[q ^ low], dr=low)
-        totals = list(totals.values())
-        return scale(pruned, totals, order)
+        bit = n_row // 2
+        while bit:
+            tot = tot + send(tot, dr=bit)
+            bit //= 2
+        return scale(pruned, [tot], order)
 
     def full():
         return dense_path(values, tile_mask, keep_mask, thr_index, n_row, n_col)

time: 98.9 us -> 98.2 us (level)
    ppermute x30 -> x29, waiting for transfers between devices: 46.3 us -> 45.8 us  [send(): return lax.ppermute(x, AXES, pairs)]
    ppermute x30 -> x29, starting transfers between devices: 35.3 us -> 35 us  [send(): return lax.ppermute(x, AXES, pairs)]
  transfers between devices with their start and end apart: 30 -> 29, of which waited for: 12 -> 11; matrix products, arithmetic and copies ran while one was open for 0% -> 0% of each run, Pallas kernels for 12% -> 12%
where the time goes in v1:
time: 98.2 us; the launch traced here: 98 us
  waiting for transfers between devices  45.8 us (47%)
  starting transfers between devices  35 us (36%)
  Pallas kernels  16.3 us (17%)
    ppermute x29, waiting for transfers between devices, send(): return lax.ppermute(x, AXES, pairs)  45.8 us
    ppermute x29, starting transfers between devices, send(): return lax.ppermute(x, AXES, pairs)  35 us
    pallas_call x3, Pallas kernels, add_products(): pl.pallas_call(kernel, out_shape=jax.ShapeDtypeStruct((rows, cols), F32),...  6.2 us
    pallas_call x1, Pallas kernels, panel(): pl.pallas_call(functools.partial(panel_kernel, n, rows), out_shape=(jax.S...  3.38 us
  transfers between devices with their start and end apart: 29, of which 11 were waited for; matrix products, arithmetic and copies ran while one was open for 0% of the time, Pallas kernels for 12%

profile of v1, /device:TPU:0, one launch (start us, length us, event | category | flops | bytes accessed | tf_op | source)
XLA Modules:
  0.0 98.0 jit_solution(3830162787738473238)
XLA Ops:
  0.0 1.5 %pack.1 = (bf16[2064,128]{1,0:T(8,128)(2,1)S(1)}, bf16[1296,128]{1,0:T(8,128)(2,1)S(1)}) custom-call(s32[4,8]{1,0:T(4,128)} %bitcast.29, bf16[1024,512]{1,0:T(8,128)(2,1)} %block_ref.1), custom_call_target="tpu_custom_call" | custom-call | flops 1000000 | bytes 2097152 | tf_op jit(solution)/shard_map/pack/pallas_call | solution.py:85
  2.1 2.6 %collective-permute-start.15 = (bf16[1296,128]{1,0:T(8,128)(2,1)S(1)}, bf16[1296,128]{1,0:T(8,128)(2,1)S(1)}, u32[]{:S(2)}, u32[]{:S(2)}) collective-permute-start(bf16[1296,128]{1,0:T(8,128)(2,1)S(1)} %get-tuple-element.300.rest_ref.refs_1_), channel_id=1, source_target_pairs={{0,16},{1,17},{2,18},{3,19},{4,20},{5,21},{6,22},{7,23},{8,24},{9,... | collective-permute-start | bytes 995336 | tf_op jit(solution)/shard_map/ppermute | solution.py:528
  6.7 2.6 %collective-permute-start.19 = (bf16[2064,128]{1,0:T(8,128)(2,1)S(1)}, bf16[2064,128]{1,0:T(8,128)(2,1)S(1)}, u32[]{:S(2)}, u32[]{:S(2)}) collective-permute-start(bf16[2064,128]{1,0:T(8,128)(2,1)S(1)} %get-tuple-element.302.refs_0_), channel_id=1, source_target_pairs={{0,4},{1,5},{2,6},{3,7},{4,0},{5,1},{6,2},{7,3},{8,12},{9,13},{10,... | collective-permute-start | bytes 1585160 | tf_op jit(solution)/shard_map/ppermute | solution.py:528
  9.3 1.5 %pool.1 = (bf16[768,128]{1,0:T(8,128)(2,1)S(1)}, f32[8,128]{1,0:T(8,128)S(1)}) custom-call(s32[4,8]{1,0:T(4,128)} %bitcast.30, bf16[1024,512]{1,0:T(8,128)(2,1)} %block_ref.1, bf16[1296,128]{1,0:T(8,128)(2,1)S(1)} %get-tuple-element.300.rest_ref.refs_1_, bf16[1296,128]{1,0:T(8,128)(2,1)S(1)} %collective-permute-done.4.other_ref.refs_9_), custom_call_target="tpu_custom_call" | custom-call | flops 1000000 | bytes 2097152 | tf_op jit(solution)/shard_map/pool/pallas_call | solution.py:139
  10.8 1.6 %collective-permute-start.5 = (f32[8,128]{1,0:T(8,128)S(1)}, f32[8,128]{1,0:T(8,128)S(1)}, u32[]{:S(2)}, u32[]{:S(2)}) collective-permute-start(f32[8,128]{1,0:T(8,128)S(1)} %get-tuple-element.301.refs_0_), channel_id=1, source_target_pairs={{0,8},{1,9},{2,10},{3,11},{4,12},{5,13},{6,14},{7,15},{8,0},{9,1},... | collective-permute-start | bytes 12296 | tf_op jit(solution)/shard_map/ppermute | solution.py:528
  13.1 1.7 %collective-permute-start.6 = (f32[8,128]{1,0:T(8,128)S(1)}, f32[8,128]{1,0:T(8,128)S(1)}, u32[]{:S(2)}, u32[]{:S(2)}) collective-permute-start(f32[8,128]{1,0:T(8,128)S(1)} %get-tuple-element.301.refs_0_), channel_id=1, source_target_pairs={{0,16},{1,17},{2,18},{3,19},{4,20},{5,21},{6,22},{7,23},{8,24},{9,... | collective-permute-start | bytes 12296 | tf_op jit(solution)/shard_map/ppermute | solution.py:528
  14.8 11.1 %collective-permute-done.5.refs_1_ = f32[8,128]{1,0:T(8,128)S(1)} collective-permute-done((f32[8,128]{1,0:T(8,128)S(1)}, f32[8,128]{1,0:T(8,128)S(1)}, u32[]{:S(2)}, u32[]{:S(2)}) %collective-permute-start.5) | collective-permute-done | bytes 4128 | tf_op jit(solution)/shard_map/ppermute | solution.py:528
  28.9 1.7 %collective-permute-done.7.refs_3_ = f32[8,128]{1,0:T(8,128)S(1)} collective-permute-done((f32[8,128]{1,0:T(8,128)S(1)}, f32[8,128]{1,0:T(8,128)S(1)}, u32[]{:S(2)}, u32[]{:S(2)}) %collective-permute-start.7) | collective-permute-done | bytes 4128 | tf_op jit(solution)/shard_map/ppermute | solution.py:528
  32.5 1.6 %collective-permute-start.25 = (bf16[2064,128]{1,0:T(8,128)(2,1)S(1)}, bf16[2064,128]{1,0:T(8,128)(2,1)S(1)}, u32[]{:S(2)}, u32[]{:S(2)}) collective-permute-start(bf16[2064,128]{1,0:T(8,128)(2,1)S(1)} %get-tuple-element.302.refs_0_), channel_id=1, source_target_pairs={{0,2},{1,3},{2,0},{3,1},{4,6},{5,7},{6,4},{7,5},{8,10},{9,11},{10,... | collective-permute-start | bytes 1585160 | tf_op jit(solution)/shard_map/ppermute | solution.py:528
  34.0 2.6 %collective-permute-start.22 = (bf16[768,128]{1,0:T(8,128)(2,1)S(1)}, bf16[768,128]{1,0:T(8,128)(2,1)S(1)}, u32[]{:S(2)}, u32[]{:S(2)}) collective-permute-start(bf16[768,128]{1,0:T(8,128)(2,1)S(1)} %get-tuple-element.305), channel_id=1, source_target_pairs={{0,4},{1,5},{2,6},{3,7},{4,0},{5,1},{6,2},{7,3},{8,12},{9,13},{10,... | collective-permute-start | bytes 589832 | tf_op jit(solution)/shard_map/ppermute | solution.py:528
  37.1 3.3 %collective-permute-done.14.refs_4_ = bf16[2064,128]{1,0:T(8,128)(2,1)S(1)} collective-permute-done((bf16[2064,128]{1,0:T(8,128)(2,1)S(1)}, bf16[2064,128]{1,0:T(8,128)(2,1)S(1)}, u32[]{:S(2)}, u32[]{:S(2)}) %collective-permute-start.14) | collective-permute-done | bytes 528416 | tf_op jit(solution)/shard_map/ppermute | solution.py:528
  42.4 8.2 %collective-permute-done.22.refs_6_ = bf16[768,128]{1,0:T(8,128)(2,1)S(1)} collective-permute-done((bf16[768,128]{1,0:T(8,128)(2,1)S(1)}, bf16[768,128]{1,0:T(8,128)(2,1)S(1)}, u32[]{:S(2)}, u32[]{:S(2)}) %collective-permute-start.22) | collective-permute-done | bytes 196640 | tf_op jit(solution)/shard_map/ppermute | solution.py:528
  50.7 3.5 %collective-permute-start.27 = (bf16[768,128]{1,0:T(8,128)(2,1)S(1)}, bf16[768,128]{1,0:T(8,128)(2,1)S(1)}, u32[]{:S(2)}, u32[]{:S(2)}) collective-permute-start(bf16[768,128]{1,0:T(8,128)(2,1)S(1)} %get-tuple-element.305), channel_id=1, source_target_pairs={{0,2},{1,3},{2,0},{3,1},{4,6},{5,7},{6,4},{7,5},{8,10},{9,11},{10,... | collective-permute-start | bytes 589832 | tf_op jit(solution)/shard_map/ppermute | solution.py:528
  54.1 12.1 %collective-permute-done.27.refs_2_ = bf16[768,128]{1,0:T(8,128)(2,1)S(1)} collective-permute-done((bf16[768,128]{1,0:T(8,128)(2,1)S(1)}, bf16[768,128]{1,0:T(8,128)(2,1)S(1)}, u32[]{:S(2)}, u32[]{:S(2)}) %collective-permute-start.27) | collective-permute-done | bytes 196640 | tf_op jit(solution)/shard_map/ppermute | solution.py:528
  67.3 1.9 %collective-permute-done.30.refs_7_ = bf16[768,128]{1,0:T(8,128)(2,1)S(1)} collective-permute-done((bf16[768,128]{1,0:T(8,128)(2,1)S(1)}, bf16[768,128]{1,0:T(8,128)(2,1)S(1)}, u32[]{:S(2)}, u32[]{:S(2)}) %collective-permute-start.30) | collective-permute-done | bytes 196640 | tf_op jit(solution)/shard_map/ppermute | solution.py:528
  69.2 1.6 %collective-permute-start.23 = (bf16[768,128]{1,0:T(8,128)(2,1)S(1)}, bf16[768,128]{1,0:T(8,128)(2,1)S(1)}, u32[]{:S(2)}, u32[]{:S(2)}) collective-permute-start(bf16[768,128]{1,0:T(8,128)(2,1)S(1)} %collective-permute-done.22.refs_6_), channel_id=1, source_target_pairs={{0,2},{1,3},{2,0},{3,1},{4,6},{5,7},{6,4},{7,5},{8,10},{9,11},{10,... | collective-permute-start | bytes 589832 | tf_op jit(solution)/shard_map/ppermute | solution.py:528
  70.8 3.4 %panel.1 = (bf16[4096,512]{1,0:T(8,128)(2,1)S(1)}, f32[1024,512]{1,0:T(8,128)S(1)}) custom-call(bf16[2064,128]{1,0:T(8,128)(2,1)S(1)} %get-tuple-element.302.refs_0_, bf16[1296,128]{1,0:T(8,128)(2,1)S(1)} %get-tuple-element.300.rest_ref.refs_1_, bf16[2064,128]{1,0:T(8,128)(2,1)S(1)} %collective-permute-done.12.refs_2_, ...), custom_call_target="tpu_custom_call" | custom-call | flops 1073741824 | bytes 8388608 | tf_op jit(solution)/shard_map/panel/pallas_call | solution.py:305
  74.2 2.6 %collective-permute-start.10 = (f32[16,128]{1,0:T(8,128)S(1)}, f32[16,128]{1,0:T(8,128)S(1)}, u32[]{:S(2)}, u32[]{:S(2)}) collective-permute-start(f32[16,128]{1,0:T(8,128)S(1)} %pad_maximum_fusion.refs_0_), channel_id=1, source_target_pairs={{0,4},{1,5},{2,6},{3,7},{4,0},{5,1},{6,2},{7,3},{8,12},{9,13},{10,... | collective-permute-start | bytes 24584 | tf_op jit(solution)/shard_map/ppermute | solution.py:528
  76.8 2.9 %collective-permute-start.11 = (f32[16,128]{1,0:T(8,128)S(1)}, f32[16,128]{1,0:T(8,128)S(1)}, u32[]{:S(2)}, u32[]{:S(2)}) collective-permute-start(f32[16,128]{1,0:T(8,128)S(1)} %pad_maximum_fusion.refs_0_), channel_id=1, source_target_pairs={{0,6},{1,7},{2,4},{3,5},{4,2},{5,3},{6,0},{7,1},{8,14},{9,15},{10,... | collective-permute-start | bytes 24584 | tf_op jit(solution)/shard_map/ppermute | solution.py:528
  79.9 3.3 %dots.3.prior_ref = f32[1024,512]{1,0:T(8,128)S(1)} custom-call(bf16[2064,128]{1,0:T(8,128)(2,1)S(1)} %collective-permute-done.25.refs_0_, bf16[2064,128]{1,0:T(8,128)(2,1)S(1)} %collective-permute-done.26.refs_1_, bf16[768,128]{1,0:T(8,128)(2,1)S(1)} %collective-permute-done.27.refs_2_, ...), custom_call_target="tpu_custom_call", output_to_operand_aliasing={{}: (9, {})} | custom-call | flops 2147483648 | bytes 6291456 | tf_op jit(solution)/shard_map/dots/pallas_call | solution.py:337
  88.1 9.9 %conditional.1 = (bf16[1024,512]{1,0:T(8,128)(2,1)}) conditional(s32[]{:T(128)} %bitcast.3, (f32[8,4]{0,1:T(4,128)S(1)}, bf16[2064,128]{1,0:T(8,128)(2,1)S(1)}, bf16[2064,128]{1,0:T(8,128)(2,1)S(1)}, bf16[768,128]{1,0:T(8,128)(2,1)S(1)}, bf16[768,128]{1,0:T(8,128)(2,1)S(1)}, /*index=5*/bf16[4096,512]{1,0:T(8,128)(2,1)S(1)}, ...), branch_computations={%region_0.0_spmd, %region_1.10_spmd} | conditional | flops 1074791424 | bytes 55080728 | solution.py:578
  90.2 3.1 %collective-permute-done = f32[1,512]{1,0:T(1,128)S(1)} collective-permute-done((f32[1,512]{1,0:T(1,128)S(1)}, f32[1,512]{1,0:T(1,128)S(1)}, u32[]{:S(2)}, u32[]{:S(2)}) %collective-permute-start) | collective-permute-done | bytes 2080 | tf_op jit(solution)/shard_map/cond/branch_0_fun/ppermute | solution.py:528
  93.3 1.5 %collective-permute-start.1 = (f32[1,512]{1,0:T(1,128)S(1)}, f32[1,512]{1,0:T(1,128)S(1)}, u32[]{:S(2)}, u32[]{:S(2)}) collective-permute-start(f32[1,512]{1,0:T(1,128)S(1)} %add.92), channel_id=1, source_target_pairs={{0,8},{1,9},{2,10},{3,11},{4,12},{5,13},{6,14},{7,15},{8,0},{9,1},... | collective-permute-start | bytes 6152 | tf_op jit(solution)/shard_map/cond/branch_0_fun/ppermute | solution.py:528
  94.8 2.1 %collective-permute-done.1 = f32[1,512]{1,0:T(1,128)S(1)} collective-permute-done((f32[1,512]{1,0:T(1,128)S(1)}, f32[1,512]{1,0:T(1,128)S(1)}, u32[]{:S(2)}, u32[]{:S(2)}) %collective-permute-start.1) | collective-permute-done | bytes 2080 | tf_op jit(solution)/shard_map/cond/branch_0_fun/ppermute | solution.py:528
  (58 shorter events, 19.2 us)
Async XLA Ops:
  1.5 7.7 %collective-permute-start.4 = (bf16[1296,128]{1,0:T(8,128)(2,1)S(1)}, bf16[1296,128]{1,0:T(8,128)(2,1)S(1)}, u32[]{:S(2)}, u32[]{:S(2)}) collective-permute-start(bf16[1296,128]{1,0:T(8,128)(2,1)S(1)} %get-tuple-element.300.rest_ref.refs_1_), channel_id=1, source_target_pairs={{0,1},{1,0},{2,3},{3,2},{4,5},{5,4},{6,7},{7,6},{8,9},{9,8},{10,11... | collective-permute-start | bytes 995336 | tf_op jit(solution)/shard_map/ppermute | solution.py:528
  2.1 11.0 %collective-permute-start.15 = (bf16[1296,128]{1,0:T(8,128)(2,1)S(1)}, bf16[1296,128]{1,0:T(8,128)(2,1)S(1)}, u32[]{:S(2)}, u32[]{:S(2)}) collective-permute-start(bf16[1296,128]{1,0:T(8,128)(2,1)S(1)} %get-tuple-element.300.rest_ref.refs_1_), channel_id=1, source_target_pairs={{0,16},{1,17},{2,18},{3,19},{4,20},{5,21},{6,22},{7,23},{8,24},{9,... | collective-permute-start | bytes 995336 | tf_op jit(solution)/shard_map/ppermute | solution.py:528
  4.7 29.4 %collective-permute-start.12 = (bf16[2064,128]{1,0:T(8,128)(2,1)S(1)}, bf16[2064,128]{1,0:T(8,128)(2,1)S(1)}, u32[]{:S(2)}, u32[]{:S(2)}) collective-permute-start(bf16[2064,128]{1,0:T(8,128)(2,1)S(1)} %get-tuple-element.302.refs_0_), channel_id=1, source_target_pairs={{0,8},{1,9},{2,10},{3,11},{4,12},{5,13},{6,14},{7,15},{8,0},{9,1},... | collective-permute-start | bytes 1585160 | tf_op jit(solution)/shard_map/ppermute | solution.py:528
  6.2 24.4 %collective-permute-start.13 = (bf16[1296,128]{1,0:T(8,128)(2,1)S(1)}, bf16[1296,128]{1,0:T(8,128)(2,1)S(1)}, u32[]{:S(2)}, u32[]{:S(2)}) collective-permute-start(bf16[1296,128]{1,0:T(8,128)(2,1)S(1)} %get-tuple-element.300.rest_ref.refs_1_), channel_id=1, source_target_pairs={{0,8},{1,9},{2,10},{3,11},{4,12},{5,13},{6,14},{7,15},{8,0},{9,1},... | collective-permute-start | bytes 995336 | tf_op jit(solution)/shard_map/ppermute | solution.py:528
  6.7 29.9 %collective-permute-start.19 = (bf16[2064,128]{1,0:T(8,128)(2,1)S(1)}, bf16[2064,128]{1,0:T(8,128)(2,1)S(1)}, u32[]{:S(2)}, u32[]{:S(2)}) collective-permute-start(bf16[2064,128]{1,0:T(8,128)(2,1)S(1)} %get-tuple-element.302.refs_0_), channel_id=1, source_target_pairs={{0,4},{1,5},{2,6},{3,7},{4,0},{5,1},{6,2},{7,3},{8,12},{9,13},{10,... | collective-permute-start | bytes 1585160 | tf_op jit(solution)/shard_map/ppermute | solution.py:528
  10.8 15.1 %collective-permute-start.5 = (f32[8,128]{1,0:T(8,128)S(1)}, f32[8,128]{1,0:T(8,128)S(1)}, u32[]{:S(2)}, u32[]{:S(2)}) collective-permute-start(f32[8,128]{1,0:T(8,128)S(1)} %get-tuple-element.301.refs_0_), channel_id=1, source_target_pairs={{0,8},{1,9},{2,10},{3,11},{4,12},{5,13},{6,14},{7,15},{8,0},{9,1},... | collective-permute-start | bytes 12296 | tf_op jit(solution)/shard_map/ppermute | solution.py:528
  13.1 14.3 %collective-permute-start.6 = (f32[8,128]{1,0:T(8,128)S(1)}, f32[8,128]{1,0:T(8,128)S(1)}, u32[]{:S(2)}, u32[]{:S(2)}) collective-permute-start(f32[8,128]{1,0:T(8,128)S(1)} %get-tuple-element.301.refs_0_), channel_id=1, source_target_pairs={{0,16},{1,17},{2,18},{3,19},{4,20},{5,21},{6,22},{7,23},{8,24},{9,... | collective-permute-start | bytes 12296 | tf_op jit(solution)/shard_map/ppermute | solution.py:528
  26.0 4.6 %collective-permute-start.7 = (f32[8,128]{1,0:T(8,128)S(1)}, f32[8,128]{1,0:T(8,128)S(1)}, u32[]{:S(2)}, u32[]{:S(2)}) collective-permute-start(f32[8,128]{1,0:T(8,128)S(1)} %get-tuple-element.301.refs_0_), channel_id=1, source_target_pairs={{0,24},{1,25},{2,26},{3,27},{4,28},{5,29},{6,30},{7,31},{8,16},{9,... | collective-permute-start | bytes 12296 | tf_op jit(solution)/shard_map/ppermute | solution.py:528
  27.4 13.0 %collective-permute-start.14 = (bf16[2064,128]{1,0:T(8,128)(2,1)S(1)}, bf16[2064,128]{1,0:T(8,128)(2,1)S(1)}, u32[]{:S(2)}, u32[]{:S(2)}) collective-permute-start(bf16[2064,128]{1,0:T(8,128)(2,1)S(1)} %get-tuple-element.302.refs_0_), channel_id=1, source_target_pairs={{0,16},{1,17},{2,18},{3,19},{4,20},{5,21},{6,22},{7,23},{8,24},{9,... | collective-permute-start | bytes 1585160 | tf_op jit(solution)/shard_map/ppermute | solution.py:528
  30.6 10.4 %collective-permute-start.18 = (bf16[2064,128]{1,0:T(8,128)(2,1)S(1)}, bf16[2064,128]{1,0:T(8,128)(2,1)S(1)}, u32[]{:S(2)}, u32[]{:S(2)}) collective-permute-start(bf16[2064,128]{1,0:T(8,128)(2,1)S(1)} %get-tuple-element.302.refs_0_), channel_id=1, source_target_pairs={{0,1},{1,0},{2,3},{3,2},{4,5},{5,4},{6,7},{7,6},{8,9},{9,8},{10,11... | collective-permute-start | bytes 1585160 | tf_op jit(solution)/shard_map/ppermute | solution.py:528
  32.5 33.8 %collective-permute-start.25 = (bf16[2064,128]{1,0:T(8,128)(2,1)S(1)}, bf16[2064,128]{1,0:T(8,128)(2,1)S(1)}, u32[]{:S(2)}, u32[]{:S(2)}) collective-permute-start(bf16[2064,128]{1,0:T(8,128)(2,1)S(1)} %get-tuple-element.302.refs_0_), channel_id=1, source_target_pairs={{0,2},{1,3},{2,0},{3,1},{4,6},{5,7},{6,4},{7,5},{8,10},{9,11},{10,... | collective-permute-start | bytes 1585160 | tf_op jit(solution)/shard_map/ppermute | solution.py:528
  34.0 16.6 %collective-permute-start.22 = (bf16[768,128]{1,0:T(8,128)(2,1)S(1)}, bf16[768,128]{1,0:T(8,128)(2,1)S(1)}, u32[]{:S(2)}, u32[]{:S(2)}) collective-permute-start(bf16[768,128]{1,0:T(8,128)(2,1)S(1)} %get-tuple-element.305), channel_id=1, source_target_pairs={{0,4},{1,5},{2,6},{3,7},{4,0},{5,1},{6,2},{7,3},{8,12},{9,13},{10,... | collective-permute-start | bytes 589832 | tf_op jit(solution)/shard_map/ppermute | solution.py:528
  36.6 30.3 %collective-permute-start.20 = (bf16[2064,128]{1,0:T(8,128)(2,1)S(1)}, bf16[2064,128]{1,0:T(8,128)(2,1)S(1)}, u32[]{:S(2)}, u32[]{:S(2)}) collective-permute-start(bf16[2064,128]{1,0:T(8,128)(2,1)S(1)} %collective-permute-done.19.refs_4_), channel_id=1, source_target_pairs={{0,2},{1,3},{2,0},{3,1},{4,6},{5,7},{6,4},{7,5},{8,10},{9,11},{10,... | collective-permute-start | bytes 1585160 | tf_op jit(solution)/shard_map/ppermute | solution.py:528
  40.4 26.4 %collective-permute-start.17 = (bf16[1296,128]{1,0:T(8,128)(2,1)S(1)}, bf16[1296,128]{1,0:T(8,128)(2,1)S(1)}, u32[]{:S(2)}, u32[]{:S(2)}) collective-permute-start(bf16[1296,128]{1,0:T(8,128)(2,1)S(1)} %collective-permute-done.15.refs_5_), channel_id=1, source_target_pairs={{0,8},{1,9},{2,10},{3,11},{4,12},{5,13},{6,14},{7,15},{8,0},{9,1},... | collective-permute-start | bytes 995336 | tf_op jit(solution)/shard_map/ppermute | solution.py:528
  40.9 29.9 %collective-permute-start.16 = (bf16[2064,128]{1,0:T(8,128)(2,1)S(1)}, bf16[2064,128]{1,0:T(8,128)(2,1)S(1)}, u32[]{:S(2)}, u32[]{:S(2)}) collective-permute-start(bf16[2064,128]{1,0:T(8,128)(2,1)S(1)} %collective-permute-done.12.refs_2_), channel_id=1, source_target_pairs={{0,16},{1,17},{2,18},{3,19},{4,20},{5,21},{6,22},{7,23},{8,24},{9,... | collective-permute-start | bytes 1585160 | tf_op jit(solution)/shard_map/ppermute | solution.py:528
  50.7 15.6 %collective-permute-start.27 = (bf16[768,128]{1,0:T(8,128)(2,1)S(1)}, bf16[768,128]{1,0:T(8,128)(2,1)S(1)}, u32[]{:S(2)}, u32[]{:S(2)}) collective-permute-start(bf16[768,128]{1,0:T(8,128)(2,1)S(1)} %get-tuple-element.305), channel_id=1, source_target_pairs={{0,2},{1,3},{2,0},{3,1},{4,6},{5,7},{6,4},{7,5},{8,10},{9,11},{10,... | collective-permute-start | bytes 589832 | tf_op jit(solution)/shard_map/ppermute | solution.py:528
  66.3 13.5 %collective-permute-start.29 = (bf16[2064,128]{1,0:T(8,128)(2,1)S(1)}, bf16[2064,128]{1,0:T(8,128)(2,1)S(1)}, u32[]{:S(2)}, u32[]{:S(2)}) collective-permute-start(bf16[2064,128]{1,0:T(8,128)(2,1)S(1)} %collective-permute-done.19.refs_4_), channel_id=1, source_target_pairs={{0,1},{1,0},{2,3},{3,2},{4,5},{5,4},{6,7},{7,6},{8,9},{9,8},{10,11... | collective-permute-start | bytes 1585160 | tf_op jit(solution)/shard_map/ppermute | solution.py:528
  66.3 13.5 %collective-permute-start.26 = (bf16[2064,128]{1,0:T(8,128)(2,1)S(1)}, bf16[2064,128]{1,0:T(8,128)(2,1)S(1)}, u32[]{:S(2)}, u32[]{:S(2)}) collective-permute-start(bf16[2064,128]{1,0:T(8,128)(2,1)S(1)} %collective-permute-done.25.refs_0_), channel_id=1, source_target_pairs={{0,1},{1,0},{2,3},{3,2},{4,5},{5,4},{6,7},{7,6},{8,9},{9,8},{10,11... | collective-permute-start | bytes 1585160 | tf_op jit(solution)/shard_map/ppermute | solution.py:528
  66.9 19.8 %collective-permute-start.21 = (bf16[2064,128]{1,0:T(8,128)(2,1)S(1)}, bf16[2064,128]{1,0:T(8,128)(2,1)S(1)}, u32[]{:S(2)}, u32[]{:S(2)}) collective-permute-start(bf16[2064,128]{1,0:T(8,128)(2,1)S(1)} %collective-permute-done.20.head_ref), channel_id=1, source_target_pairs={{0,1},{1,0},{2,3},{3,2},{4,5},{5,4},{6,7},{7,6},{8,9},{9,8},{10,11... | collective-permute-start | bytes 1585160 | tf_op jit(solution)/shard_map/ppermute | solution.py:528
  69.2 7.6 %collective-permute-start.23 = (bf16[768,128]{1,0:T(8,128)(2,1)S(1)}, bf16[768,128]{1,0:T(8,128)(2,1)S(1)}, u32[]{:S(2)}, u32[]{:S(2)}) collective-permute-start(bf16[768,128]{1,0:T(8,128)(2,1)S(1)} %collective-permute-done.22.refs_6_), channel_id=1, source_target_pairs={{0,2},{1,3},{2,0},{3,1},{4,6},{5,7},{6,4},{7,5},{8,10},{9,11},{10,... | collective-permute-start | bytes 589832 | tf_op jit(solution)/shard_map/ppermute | solution.py:528
  74.2 9.0 %collective-permute-start.10 = (f32[16,128]{1,0:T(8,128)S(1)}, f32[16,128]{1,0:T(8,128)S(1)}, u32[]{:S(2)}, u32[]{:S(2)}) collective-permute-start(f32[16,128]{1,0:T(8,128)S(1)} %pad_maximum_fusion.refs_0_), channel_id=1, source_target_pairs={{0,4},{1,5},{2,6},{3,7},{4,0},{5,1},{6,2},{7,3},{8,12},{9,13},{10,... | collective-permute-start | bytes 24584 | tf_op jit(solution)/shard_map/ppermute | solution.py:528
  76.8 6.3 %collective-permute-start.11 = (f32[16,128]{1,0:T(8,128)S(1)}, f32[16,128]{1,0:T(8,128)S(1)}, u32[]{:S(2)}, u32[]{:S(2)}) collective-permute-start(f32[16,128]{1,0:T(8,128)S(1)} %pad_maximum_fusion.refs_0_), channel_id=1, source_target_pairs={{0,6},{1,7},{2,4},{3,5},{4,2},{5,3},{6,0},{7,1},{8,14},{9,15},{10,... | collective-permute-start | bytes 24584 | tf_op jit(solution)/shard_map/ppermute | solution.py:528
  79.8 3.7 %collective-permute-start.9 = (f32[16,128]{1,0:T(8,128)S(1)}, f32[16,128]{1,0:T(8,128)S(1)}, u32[]{:S(2)}, u32[]{:S(2)}) collective-permute-start(f32[16,128]{1,0:T(8,128)S(1)} %pad_maximum_fusion.refs_0_), channel_id=1, source_target_pairs={{0,2},{1,3},{2,0},{3,1},{4,6},{5,7},{6,4},{7,5},{8,10},{9,11},{10,... | collective-permute-start | bytes 24584 | tf_op jit(solution)/shard_map/ppermute | solution.py:528
  79.8 8.3 %collective-permute-start.24 = (bf16[768,128]{1,0:T(8,128)(2,1)S(1)}, bf16[768,128]{1,0:T(8,128)(2,1)S(1)}, u32[]{:S(2)}, u32[]{:S(2)}) collective-permute-start(bf16[768,128]{1,0:T(8,128)(2,1)S(1)} %collective-permute-done.23), channel_id=1, source_target_pairs={{0,1},{1,0},{2,3},{3,2},{4,5},{5,4},{6,7},{7,6},{8,9},{9,8},{10,11... | collective-permute-start | bytes 589832 | tf_op jit(solution)/shard_map/ppermute | solution.py:528
  (9 other events, 88.9 us)
